TPU v7x, 32 devices: a whole 2x2x4 slice. The times are simulated.
32 devices in a mesh: row: 8 (over z, y), col: 4 (over x, core).
Axes of the slice: x: 2, y: 2, z: 4, core: 2. Of those that a mesh axis runs over, the one named last changes fastest.
Arguments:
- image_in: bfloat16 [2048, 1536], P('row', 'col'), may hold values from -6 to 6
- text_in: bfloat16 [2464, 1536], P('row', 'col'), may hold values from -6 to 6
- condition: bfloat16 [16, 1536], P(None, 'row'), may hold values from -6 to 6
- ranges: int32 [16, 2], P('row'), may hold values from 0 to 192, as said below
- mod_weight: bfloat16 [1, 1536, 2, 6, 1536], P(None, 'row', None, None, 'col'), may hold values from -0.15625 to 0.15625
- qkv_weight: bfloat16 [1, 1536, 2, 3, 1536], P(None, 'row', None, None, 'col'), may hold values from -0.15625 to 0.15625
- out_weight: bfloat16 [1, 1536, 2, 1536], P(None, 'row', None, 'col'), may hold values from -2.5 to 2.5
- up_weight: bfloat16 [1, 1536, 2, 6144], P(None, 'row', None, 'col'), may hold values from -0.15625 to 0.15625
- down_weight: bfloat16 [1, 1536, 2, 6144], P(None, 'row', None, 'col'), may hold values from -0.078125 to 0.078125
- image_cot: bfloat16 [2048, 1536], P('row', 'col'), may hold values from -6 to 6
- text_cot: bfloat16 [2464, 1536], P('row', 'col'), may hold values from -6 to 6
Outputs:
- image_out: float32 [2048, 1536], P('row', 'col')
- text_out: float32 [2464, 1536], P('row', 'col')
- grad_image: float32 [2048, 1536], P('row', 'col')
- grad_text: float32 [2464, 1536], P('row', 'col')
- grad_cond: float32 [16, 1536], P(None, 'row')
- grad_mod: float32 [1, 1536, 2, 6, 1536], P(None, 'row', None, None, 'col')
- grad_qkv: float32 [1, 1536, 2, 3, 1536], P(None, 'row', None, None, 'col')
- grad_out: float32 [1, 1536, 2, 1536], P(None, 'row', None, 'col')
- grad_up: float32 [1, 1536, 2, 6144], P(None, 'row', None, 'col')
- grad_down: float32 [1, 1536, 2, 6144], P(None, 'row', None, 'col')
Inputs may be any that keep to these rules, and one draw needn't show every extreme that they name: `ranges`: each index of row has 2 slots; the first always holds 154 text rows and a multiple of 64 image rows; the second is empty or holds 154 text rows and exactly the image rows the first leaves over, so that index's 256 image rows are full.
All inputs are finite; a program needn't handle non-finite values.
Results may differ from a plain program's by a relative error of at most 0.015.
The roundings to bfloat16 on the way count: a program that leaves them out, or rounds other values in their place, can miss the bound.
Values may be sent and summed in bfloat16 or wider, within the bound.
A program may use at most 320 MiB of HBM per device.

v0:
```python
import math
import jax
import jax.numpy as jnp
from jax import lax
from jax.sharding import PartitionSpec as P

D = 1536
LAYERS = 1
IMG_DEV = 256
HD = 64
TXT_DEV = 308
EPSILON = 1e-06
HIGHEST = lax.Precision.HIGHEST


def slot_table(lengths, image_rows, text_rows):
    ends = jnp.cumsum(lengths, axis=0, dtype=jnp.int32)
    starts = ends - lengths
    slot_ids = jnp.arange(lengths.shape[0], dtype=jnp.int32)
    tables = []
    segments = []
    for column, amount in ((0, image_rows), (1, text_rows)):
        places = jnp.arange(amount, dtype=jnp.int32)[:, None]
        inside = ((places >= starts[None, :, column]) & (places < ends[None, :, column])).astype(
            jnp.int32
        )
        tables.append(inside.astype(jnp.float32))
        filled = jnp.sum(inside, axis=1, dtype=jnp.int32)
        segments.append(
            jnp.sum(inside * slot_ids[None, :], axis=1, dtype=jnp.int32)
            + lengths.shape[0] * (1 - filled)
        )
    return (jnp.concatenate(tables, axis=0), jnp.concatenate(segments, axis=0))


def stream_dot(left, right_image, right_text):
    upper = jnp.dot(left[:IMG_DEV], right_image, preferred_element_type=jnp.float32)
    lower = jnp.dot(left[IMG_DEV:], right_text, preferred_element_type=jnp.float32)
    return jnp.concatenate([upper, lower], axis=0)


def stream_outer(left, right):
    upper = jnp.einsum(
        "nk,nf->kf", left[:IMG_DEV], right[:IMG_DEV], preferred_element_type=jnp.float32
    )
    lower = jnp.einsum(
        "nk,nf->kf", left[IMG_DEV:], right[IMG_DEV:], preferred_element_type=jnp.float32
    )
    return (upper, lower)


def row_mod(slot_ones, mod_mine, layer_index, component):
    upper = jnp.dot(slot_ones[:IMG_DEV], mod_mine[:, layer_index, 0, component], precision=HIGHEST)
    lower = jnp.dot(slot_ones[IMG_DEV:], mod_mine[:, layer_index, 1, component], precision=HIGHEST)
    return jnp.concatenate([upper, lower], axis=0)


def slot_sums(slot_ones, rows):
    upper = jnp.dot(slot_ones[:IMG_DEV].T, rows[:IMG_DEV], precision=HIGHEST)
    lower = jnp.dot(slot_ones[IMG_DEV:].T, rows[IMG_DEV:], precision=HIGHEST)
    return jnp.stack([upper, lower], axis=1)


def feature_sums(first, second):
    return lax.psum((jnp.sum(first, axis=1), jnp.sum(second, axis=1)), "col")


def normalize(hidden):
    totals, squares = feature_sums(hidden, hidden * hidden)
    center = totals / D
    spread = squares / D - center * center
    scaling = lax.rsqrt(spread + EPSILON)
    return ((hidden - center[:, None]) * scaling[:, None], scaling[:, None])


def norm_back(grad_hat, normed, scaling):
    first, second = feature_sums(grad_hat, grad_hat * normed)
    return scaling * (grad_hat - first[:, None] / D - normed * (second[:, None] / D))


def gelu_slope(value):
    coeff = math.sqrt(2.0 / math.pi)
    tangent = jnp.tanh(coeff * (value + 0.044715 * value * value * value))
    return 0.5 * (1.0 + tangent) + 0.5 * value * (1.0 - tangent * tangent) * coeff * (
        1.0 + 3.0 * 0.044715 * value * value
    )


def silu_slope(value):
    sigma = jax.nn.sigmoid(value)
    return sigma * (1.0 + value * (1.0 - sigma))


def gather_features(values):
    return lax.all_gather(values, "col", axis=1, tiled=True)


def gather_grads(values):
    return lax.all_gather(values, "col", axis=1, tiled=True)


def scatter_features(values):
    return lax.psum_scatter(values, "col", scatter_dimension=1, tiled=True)


def scatter_back(values):
    return lax.psum_scatter(values, "col", scatter_dimension=1, tiled=True)


def spread_grads(terms, row_count):
    return lax.psum_scatter(
        terms(jnp.int32(0), row_count * lax.axis_size("row")),
        "row",
        scatter_dimension=0,
        tiled=True,
    )


def fold_rows(left, weight):
    portion = lax.all_gather(weight, "row", axis=0, tiled=True)
    return stream_dot(left, portion[:, 0], portion[:, 1])


def map_rows(left, weight):
    portion = lax.all_gather(weight, "row", axis=0, tiled=True)
    return stream_dot(left, portion[:, 0].T, portion[:, 1].T)


def apply_in(left, weight):
    result = fold_rows(left, weight)
    return result


def apply_out(left, weight):
    result = map_rows(left, weight)
    return result


def mlp_part(operands):
    grad_full, gathered, grad_lifted, activated = operands
    up_image, up_text = stream_outer(gathered, grad_lifted)
    down_image, down_text = stream_outer(grad_full, activated)
    image_part = jnp.concatenate([up_image, down_image], axis=1)
    text_part = jnp.concatenate([up_text, down_text], axis=1)
    return jnp.stack([image_part, text_part], axis=1)


def attention_part(operands):
    grad_full, gathered, grad_projected, mixed = operands
    qkv_image, qkv_text = stream_outer(gathered, grad_projected)
    out_image, out_text = stream_outer(grad_full, mixed)
    image_part = jnp.concatenate([qkv_image, out_image], axis=1)
    text_part = jnp.concatenate([qkv_text, out_text], axis=1)
    return jnp.stack([image_part, text_part], axis=1)


def attend_head(operands, segments, scale):
    queries, key_rows, value_rows = operands
    scores = jnp.dot(queries, key_rows.T, preferred_element_type=jnp.float32) * scale
    allowed = segments[:, None] == segments[None, :]
    scores = jnp.where(allowed, scores, -jnp.inf)
    highest = jnp.max(scores, axis=1, keepdims=True)
    log_total = highest + jnp.log(jnp.sum(jnp.exp(scores - highest), axis=1, keepdims=True))
    weights = jnp.exp(scores - log_total).astype(jnp.bfloat16)
    output = jnp.dot(weights, value_rows, preferred_element_type=jnp.float32).astype(jnp.bfloat16)
    return (output, log_total[:, 0])


def attend_back_head(operands, segments, scale):
    queries, key_rows, value_rows, output, grad_output, log_total = operands
    scores = jnp.dot(queries, key_rows.T, preferred_element_type=jnp.float32) * scale
    allowed = segments[:, None] == segments[None, :]
    scores = jnp.where(allowed, scores, -jnp.inf)
    probs = jnp.exp(scores - log_total[:, None])
    grad_values = jnp.dot(
        probs.astype(jnp.bfloat16).T, grad_output, preferred_element_type=jnp.float32
    )
    grad_probs = jnp.dot(grad_output, value_rows.T, preferred_element_type=jnp.float32)
    inner = jnp.sum(
        grad_output.astype(jnp.float32) * output.astype(jnp.float32), axis=1, keepdims=True
    )
    grad_scores = (probs * (grad_probs - inner) * scale).astype(jnp.bfloat16)
    grad_queries = jnp.dot(grad_scores, key_rows, preferred_element_type=jnp.float32)
    grad_keys = jnp.dot(grad_scores.T, queries, preferred_element_type=jnp.float32)
    return jnp.stack([grad_queries, grad_keys, grad_values], axis=0).astype(jnp.bfloat16)


def per_device(
    image_in,
    text_in,
    condition,
    ranges,
    mod_weight,
    qkv_weight,
    out_weight,
    up_weight,
    down_weight,
    image_cot,
    text_cot,
):
    slot_ones, segments = slot_table(ranges, IMG_DEV, TXT_DEV)
    col_width = image_in.shape[1]
    ff_width = up_weight.shape[3]
    row_count = qkv_weight.shape[1]
    heads_here = col_width // HD
    scale = 1.0 / math.sqrt(HD)
    silu_cond = jax.nn.silu(condition.astype(jnp.float32)).astype(jnp.bfloat16)
    mod_terms = jnp.einsum(
        "sd,ldxkf->slxkf", silu_cond, mod_weight, preferred_element_type=jnp.float32
    )
    mod_mine = lax.psum_scatter(mod_terms, "row", scatter_dimension=0, tiled=True)
    hidden = jnp.concatenate([image_in, text_in], axis=0).astype(jnp.float32)
    layer_index = 0
    qkv_local = qkv_weight[layer_index].reshape(row_count, 2, 3 * col_width)
    whole = (None, None, None, None)
    mods = [row_mod(slot_ones, mod_mine, layer_index, part_no) for part_no in range(6)]
    normed_one, scaling_one = normalize(hidden)
    modulated_one = (normed_one * (1.0 + mods[1]) + mods[0]).astype(jnp.bfloat16)
    gathered_one = gather_features(modulated_one)
    projected = apply_in(gathered_one, qkv_local).astype(jnp.bfloat16)
    heads_form = projected.reshape(-1, 3, heads_here, HD).transpose(1, 2, 0, 3)
    attended, log_totals = lax.map(
        lambda operands: attend_head(operands, segments, scale),
        (heads_form[0], heads_form[1], heads_form[2]),
    )
    mixed = attended.transpose(1, 0, 2).reshape(-1, col_width)
    branch_one = scatter_features(apply_out(mixed, out_weight[layer_index]))
    midway = hidden + mods[2] * branch_one
    normed_two, scaling_two = normalize(midway)
    modulated_two = (normed_two * (1.0 + mods[4]) + mods[3]).astype(jnp.bfloat16)
    gathered_two = gather_features(modulated_two)
    lifted = apply_in(gathered_two, up_weight[layer_index])
    activated = jax.nn.gelu(lifted, approximate=True).astype(jnp.bfloat16)
    branch_two = scatter_features(apply_out(activated, down_weight[layer_index]))
    hidden = midway + mods[5] * branch_two
    saved = [
        (
            whole,
            normed_one,
            scaling_one,
            gathered_one,
            heads_form,
            attended,
            log_totals,
            mixed,
            branch_one,
            normed_two,
            scaling_two,
            gathered_two,
            lifted,
            activated,
            branch_two,
        )
    ]
    image_out = hidden[:IMG_DEV]
    text_out = hidden[IMG_DEV:]
    grad_hidden = jnp.concatenate([image_cot, text_cot], axis=0).astype(jnp.float32)
    grads_qkv = [None] * LAYERS
    grads_out = [None] * LAYERS
    grads_up = [None] * LAYERS
    grads_down = [None] * LAYERS
    grads_slots = [None] * LAYERS
    for layer_index in reversed(range(LAYERS)):
        (
            whole,
            normed_one,
            scaling_one,
            gathered_one,
            heads_form,
            attended,
            log_totals,
            mixed,
            branch_one,
            normed_two,
            scaling_two,
            gathered_two,
            lifted,
            activated,
            branch_two,
        ) = saved[layer_index]
        qkv_local = qkv_weight[layer_index].reshape(row_count, 2, 3 * col_width)
        mods = [row_mod(slot_ones, mod_mine, layer_index, part_no) for part_no in range(6)]
        grad_branch_two = (grad_hidden * mods[5]).astype(jnp.bfloat16)
        gate_two_rows = grad_hidden * branch_two
        grad_full_two = gather_grads(grad_branch_two)
        grad_act = apply_in(grad_full_two, down_weight[layer_index])
        grad_lifted = (grad_act * gelu_slope(lifted)).astype(jnp.bfloat16)
        mlp_operands = (grad_full_two, gathered_two, grad_lifted, activated)
        mlp_grads = spread_grads(lambda offset, amount: mlp_part(mlp_operands), row_count)
        grads_up[layer_index] = mlp_grads[:, :, :ff_width]
        grads_down[layer_index] = mlp_grads[:, :, ff_width:]
        grad_mod_two = scatter_back(apply_out(grad_lifted, up_weight[layer_index]))
        scale_two_rows = grad_mod_two * normed_two
        grad_hidden = grad_hidden + norm_back(
            grad_mod_two * (1.0 + mods[4]), normed_two, scaling_two
        )
        grad_branch_one = (grad_hidden * mods[2]).astype(jnp.bfloat16)
        gate_one_rows = grad_hidden * branch_one
        grad_full_one = gather_grads(grad_branch_one)
        grad_mixed = apply_in(grad_full_one, out_weight[layer_index]).astype(jnp.bfloat16)
        grad_heads = grad_mixed.reshape(-1, heads_here, HD).transpose(1, 0, 2)
        grad_parts = lax.map(
            lambda operands: attend_back_head(operands, segments, scale),
            (heads_form[0], heads_form[1], heads_form[2], attended, grad_heads, log_totals),
        )
        grad_projected = grad_parts.transpose(2, 1, 0, 3).reshape(-1, 3 * col_width)
        attention_operands = (grad_full_one, gathered_one, grad_projected, mixed)
        attention_grads = spread_grads(
            lambda offset, amount: attention_part(attention_operands), row_count
        )
        grads_qkv[layer_index] = attention_grads[:, :, : 3 * col_width].reshape(
            row_count, 2, 3, col_width
        )
        grads_out[layer_index] = attention_grads[:, :, 3 * col_width :]
        grad_mod_one = scatter_back(apply_out(grad_projected, qkv_local))
        scale_one_rows = grad_mod_one * normed_one
        grad_hidden = grad_hidden + norm_back(
            grad_mod_one * (1.0 + mods[1]), normed_one, scaling_one
        )
        rows_list = [
            grad_mod_one,
            scale_one_rows,
            gate_one_rows,
            grad_mod_two,
            scale_two_rows,
            gate_two_rows,
        ]
        grads_slots[layer_index] = jnp.stack(
            [slot_sums(slot_ones, rows) for rows in rows_list], axis=2
        )
    mod_all = lax.all_gather(jnp.stack(grads_slots, axis=1), "row", axis=0, tiled=True)
    grad_mod = jnp.einsum(
        "sd,slxkf->ldxkf", silu_cond.astype(jnp.float32), mod_all, precision=HIGHEST
    )
    cond_part = jnp.einsum(
        "slxkf,ldxkf->sd", mod_all, mod_weight.astype(jnp.float32), precision=HIGHEST
    )
    cond_total = lax.psum(cond_part, "col")
    grad_cond = cond_total * silu_slope(condition.astype(jnp.float32))
    grad_image = grad_hidden[:IMG_DEV]
    grad_text = grad_hidden[IMG_DEV:]
    return (
        image_out,
        text_out,
        grad_image,
        grad_text,
        grad_cond,
        grad_mod,
        jnp.stack(grads_qkv),
        jnp.stack(grads_out),
        jnp.stack(grads_up),
        jnp.stack(grads_down),
    )


def solution(mesh):
    return jax.shard_map(
        per_device,
        mesh=mesh,
        in_specs=(
            P("row", "col"),
            P("row", "col"),
            P(None, "row"),
            P("row", None),
            P(None, "row", None, None, "col"),
            P(None, "row", None, None, "col"),
            P(None, "row", None, "col"),
            P(None, "row", None, "col"),
            P(None, "row", None, "col"),
            P("row", "col"),
            P("row", "col"),
        ),
        out_specs=(
            P("row", "col"),
            P("row", "col"),
            P("row", "col"),
            P("row", "col"),
            P(None, "row"),
            P(None, "row", None, None, "col"),
            P(None, "row", None, None, "col"),
            P(None, "row", None, "col"),
            P(None, "row", None, "col"),
            P(None, "row", None, "col"),
        ),
        check_vma=False,
    )
```

profile of v0, /device:TPU:0, one launch (start us, length us, event | category | flops | bytes accessed | tf_op | source)
XLA Modules:
  0.0 2627.9 jit_solution(4866509215842069157)
XLA Ops:
  15.9 8.5 all-reduce.6
  24.7 61.2 %all-reduce.11.cloned.1.call-done = f32[16,1,2,6,384]{4,0,3,2,1:T(8,128)} async-done(((f32[16,1,2,6,384]{4,0,3,2,1:T(8,128)}), f32[16,1,2,6,384]{4,0,3,2,1:T(8,128)}) %all-reduce.11.cloned.1.call-update) | async-done | bytes 294928
  95.3 100.8 %all-gather.15.cloned.1.call-done = bf16[1536,2,1152]{2,0,1:T(8,128)(2,1)} async-done(((bf16[192,2,1152]{2,0,1:T(8,128)(2,1)}), bf16[1536,2,1152]{2,0,1:T(8,128)(2,1)}) %all-gather.15.cloned.1.call-update) | async-done | bytes 7077904 | tf_op jit(solution)/shard_map/all_gather | solution.py:120
  196.0 6.6 slice_bitcast_fusion.13
  202.6 5.8 copy.120
  208.4 5.8 copy.119
  217.0 4.5 convolution_convert_fusion.4
  229.1 16.3 while.22
  249.0 22.4 all-gather.23.cloned.1.call-done
  297.1 17.9 reduce-scatter.6.cloned.1.call-done
  316.8 5.9 all-reduce.5
  325.0 12.6 all-gather.19.cloned.1.call-done
  337.6 140.0 %all-gather.27.cloned.1.call-done = bf16[1,1536,2,1536]{3,1,2,0:T(8,128)(2,1)} async-done(((bf16[1,192,2,1536]{3,1,2,0:T(8,128)(2,1)}), bf16[1,1536,2,1536]{3,1,2,0:T(8,128)(2,1)}) %all-gather.27.cloned.1.call-update) | async-done | bytes 9437200 | tf_op jit(solution)/shard_map/all_gather | solution.py:125
  477.7 5.2 fusion.44
  482.9 5.3 fusion.46
  488.2 127.7 %all-gather.25.cloned.1.call-done = bf16[1,1536,2,1536]{3,1,2,0:T(8,128)(2,1)} async-done(((bf16[1,192,2,1536]{3,1,2,0:T(8,128)(2,1)}), bf16[1,1536,2,1536]{3,1,2,0:T(8,128)(2,1)}) %all-gather.25.cloned.1.call-update) | async-done | bytes 9437200 | tf_op jit(solution)/shard_map/all_gather | solution.py:120
  615.9 20.9 all-gather.17.cloned.1.call-done
  636.8 4.4 fusion.43
  644.8 4.1 fusion.66
  654.3 4.1 fusion.45
  658.4 4.6 fusion.47
  665.1 29.2 %reduce-scatter.10.cloned.1.call-done = f32[564,384]{1,0:T(8,128)} async-done(((f32[564,1536]{1,0:T(8,128)}), f32[564,384]{1,0:T(8,128)}) %reduce-scatter.10.cloned.1.call-update) | async-done | bytes 866320 | tf_op jit(solution)/shard_map/reduce_scatter | solution.py:107
  696.2 6.4 all-reduce.4
  703.3 34.0 %reduce-scatter.8.cloned.1.call-done = f32[564,384]{1,0:T(8,128)} async-done(((f32[564,1536]{1,0:T(8,128)}), f32[564,384]{1,0:T(8,128)}) %reduce-scatter.8.cloned.1.call-update) | async-done | bytes 866320 | tf_op jit(solution)/shard_map/reduce_scatter | solution.py:103
  737.4 4.4 convert_multiply_fusion.2
  743.6 9.1 reduce-scatter.12.cloned.1.call-start
  759.4 4.9 all-gather.21.cloned.1.call-done
  769.1 64.8 %while.23 = (s32[]{:T(128)}, bf16[6,3,564,64]{2,3,0,1:T(8,128)(2,1)}, s32[564]{0:T(1024)}, bf16[6,564,64]{2,1,0:T(8,128)(2,1)}, bf16[6,564,64]{2,1,0:T(8,128)(2,...) while((s32[]{:T(128)}, ...), condition=%wide.region_27.28_spmd, body=%wide.region_25.27_spmd.sunk | while | flops 207346144 | bytes 8018613 | solution.py:302
  836.3 4.0 fusion.48
  849.8 4.4 fusion.132
  854.1 4.9 fusion.114
  859.0 8.2 maximum_bitcast_fusion.4
  867.3 7.8 maximum_bitcast_fusion.3
  875.0 14.7 pad_maximum_fusion.1
  889.7 28.5 %copy.139 = f32[1536,2,1536]{2,1,0:T(2,128)} copy(f32[1536,2,1536]{0,2,1:T(8,128)} %pad_maximum_fusion.1) | data formatting | bytes 37748736 | tf_op jit(solution)/shard_map/stack | solution.py:154
  921.5 5.6 fusion.122
  927.2 5.1 fusion.107
  932.2 5.1 fusion.104
  937.3 7.8 maximum_bitcast_fusion.2
  945.1 11.3 maximum_bitcast_fusion.1
  956.4 21.2 pad_maximum_fusion
  977.5 55.5 %copy.141 = f32[1536,2,3072]{2,1,0:T(2,128)} copy(f32[1536,2,3072]{0,2,1:T(8,128)} %pad_maximum_fusion) | data formatting | bytes 75497472 | tf_op jit(solution)/shard_map/stack | solution.py:145
  1054.0 33.8 %all-gather.3 = f32[16,2,6,384]{3,1,2,0:T(2,128)S(1)} all-gather(f32[2,2,6,384]{3,1,2,0:T(2,128)S(1)} %copy.135), channel_id=5, replica_groups=mesh['row'=8,'col'=4] {'row'}, dimensions={0}, use_global_device_ids=true | all-gather | bytes 331776 | tf_op jit(solution)/shard_map/all_gather | solution.py:331
  1090.0 11.9 all-reduce.3
  1107.0 4.5 copy.142
  1112.1 376.4 %all-reduce.13.cloned.1.call-done = f32[1536,2,1536]{2,1,0:T(2,128)} async-done(((f32[1536,2,1536]{2,1,0:T(2,128)}), f32[1536,2,1536]{2,1,0:T(2,128)}) %all-reduce.13.cloned.1.call-update) | async-done | bytes 18874384
  1494.4 1118.8 %all-reduce.15.cloned.1.call-done = f32[1536,2,3072]{2,1,0:T(2,128)} async-done(((f32[1536,2,3072]{2,1,0:T(2,128)}), f32[1536,2,3072]{2,1,0:T(2,128)}) %all-reduce.15.cloned.1.call-update) | async-done | bytes 37748752
  2613.2 7.8 dynamic-slice_bitcast_fusion
  (371 shorter events, 217.1 us)
Async XLA Ops:
  7.2 78.7 %all-reduce.11.cloned.1.call-start = ((), (), s32[]{:S(2)}) async-start(), calls=%async_computation.16 | async-start | bytes 589824
  10.5 185.5 %all-gather.15.cloned.1.call-start = ((), (), s32[]{:S(2)}) async-start(), calls=%async_computation.5 | async-start | bytes 7962624 | tf_op jit(solution)/shard_map/all_gather | solution.py:120
  14.3 202.7 %all-gather.13.cloned.1.call-start = ((), (), s32[]{:S(2)}) async-start(), calls=%async_computation.4 | async-start | bytes 2181120 | tf_op jit(solution)/shard_map/all_gather | solution.py:95
  24.6 264.2 %copy-start.45 = (s32[2]{0:T(128)}, s32[2]{0:T(128)S(1)}, u32[]{:S(2)}) copy-start(s32[2]{0:T(128)S(1)} %get-tuple-element.240) | copy-start | bytes 28
  24.7 264.2 %copy-start.47 = (s32[2]{0:T(128)}, s32[2]{0:T(128)S(1)}, u32[]{:S(2)}) copy-start(s32[2]{0:T(128)S(1)} %get-tuple-element.315) | copy-start | bytes 28
  24.7 270.1 %copy-start.49 = (s32[2]{0:T(128)}, s32[2]{0:T(128)S(1)}, u32[]{:S(2)}) copy-start(s32[2]{0:T(128)S(1)} %get-tuple-element.241) | copy-start | bytes 28
  24.7 270.1 %copy-start.51 = (s32[2]{0:T(128)}, s32[2]{0:T(128)S(1)}, u32[]{:S(2)}) copy-start(s32[2]{0:T(128)S(1)} %get-tuple-element.314) | copy-start | bytes 28
  24.7 68.8 %copy-start.54 = (f32[564]{0:T(1024)}, f32[564]{0:T(1024)S(1)}, u32[]{:S(2)}) copy-start(f32[564]{0:T(1024)S(1)} %get-tuple-element.312) | copy-start | bytes 6772
  24.7 68.8 %copy-start.56 = (f32[564]{0:T(1024)}, f32[564]{0:T(1024)S(1)}, u32[]{:S(2)}) copy-start(f32[564]{0:T(1024)S(1)} %get-tuple-element.313) | copy-start | bytes 6772
  85.9 7.7 copy-start.44
  93.6 177.9 %all-gather.23.cloned.1.call-start = ((), (), s32[]{:S(2)}) async-start(), calls=%async_computation.13 | async-start | bytes 2654208 | tf_op jit(solution)/shard_map/all_gather | solution.py:125
  94.4 220.6 %reduce-scatter.6.cloned.1.call-start = ((), (), s32[]{:S(2)}) async-start(), calls=%async_computation.6 | async-start | bytes 4362240 | tf_op jit(solution)/shard_map/reduce_scatter | solution.py:103
  245.4 28.9 %copy-start.17 = (bf16[6,564,64]{2,1,0:T(8,128)(2,1)}, bf16[6,564,64]{2,1,0:T(8,128)(2,1)S(1)}, u32[]{:S(2)}) copy-start(bf16[6,564,64]{2,1,0:T(8,128)(2,1)S(1)} %get-tuple-element.510) | copy-start | bytes 1299460
  245.4 28.9 %copy-start.28 = (bf16[6,564,64]{2,1,0:T(8,128)(2,1)}, bf16[6,564,64]{2,1,0:T(8,128)(2,1)S(1)}, u32[]{:S(2)}) copy-start(bf16[6,564,64]{2,1,0:T(8,128)(2,1)S(1)} %get-tuple-element.518) | copy-start | bytes 1299460
  276.4 61.2 %all-gather.19.cloned.1.call-start = ((), (), s32[]{:S(2)}) async-start(), calls=%async_computation.9 | async-start | bytes 2181120 | tf_op jit(solution)/shard_map/all_gather | solution.py:99
  281.5 196.2 %all-gather.27.cloned.1.call-start = ((), (), s32[]{:S(2)}) async-start(), calls=%async_computation.15 | async-start | bytes 10616832 | tf_op jit(solution)/shard_map/all_gather | solution.py:125
  282.7 333.2 %all-gather.25.cloned.1.call-start = ((), (), s32[]{:S(2)}) async-start(), calls=%async_computation.14 | async-start | bytes 10616832 | tf_op jit(solution)/shard_map/all_gather | solution.py:120
  285.5 351.3 %all-gather.17.cloned.1.call-start = ((), (), s32[]{:S(2)}) async-start(), calls=%async_computation.7 | async-start | bytes 2181120 | tf_op jit(solution)/shard_map/all_gather | solution.py:95
  288.9 33.8 %copy-start.14 = (f32[256,384]{1,0:T(8,128)}, f32[256,384]{1,0:T(8,128)S(1)}, u32[]{:S(2)}) copy-start(f32[256,384]{1,0:T(8,128)S(1)} %fusion.196) | copy-start | bytes 1179652
  294.8 30.1 %copy-start.7 = (f32[308,384]{1,0:T(8,128)}, f32[308,384]{1,0:T(8,128)S(1)}, u32[]{:S(2)}) copy-start(f32[308,384]{1,0:T(8,128)S(1)} %fusion.163) | copy-start | bytes 1419268
  325.0 369.3 %reduce-scatter.10.cloned.1.call-start = ((), (), s32[]{:S(2)}) async-start(), calls=%async_computation.10 | async-start | bytes 4362240 | tf_op jit(solution)/shard_map/reduce_scatter | solution.py:107
  636.8 5.4 copy-start.66
  654.2 83.1 %reduce-scatter.8.cloned.1.call-start = ((), (), s32[]{:S(2)}) async-start(), calls=%async_computation.8 | async-start | bytes 4362240 | tf_op jit(solution)/shard_map/reduce_scatter | solution.py:103
  665.1 99.2 %all-gather.21.cloned.1.call-start = ((), (), s32[]{:S(2)}) async-start(), calls=%async_computation.11 | async-start | bytes 2181120 | tf_op jit(solution)/shard_map/all_gather | solution.py:99
  694.3 43.1 %copy-start.4 = (f32[564,384]{1,0:T(8,128)S(1)}, f32[564,384]{1,0:T(8,128)}, u32[]{:S(2)}) copy-start(f32[564,384]{1,0:T(8,128)} %reduce-scatter.10.cloned.1.call-done) | copy-start | bytes 2598916
  737.4 5.3 copy-start.21
  737.4 5.3 copy-start.24
  743.6 304.8 %reduce-scatter.12.cloned.1.call-start = ((), (), s32[]{:S(2)}) async-start(), calls=%async_computation.12 | async-start | bytes 4362240 | tf_op jit(solution)/shard_map/reduce_scatter | solution.py:107
  759.4 7.3 copy-start.41
  845.6 642.9 %all-reduce.13.cloned.1.call-start = ((), (), s32[]{:S(2)}) async-start(), calls=%async_computation.17 | async-start | bytes 37748736
  918.3 1694.9 %all-reduce.15.cloned.1.call-start = ((), (), s32[]{:S(2)}) async-start(), calls=%async_computation.18 | async-start | bytes 75497472
  921.5 5.6 copy-start.13
  921.5 5.6 copy-start.34
  1033.1 7.4 copy-start.5
  1033.1 8.3 copy-start.50
  1033.2 8.3 copy-start.52
  1035.8 15.3 copy-start.9
  1035.8 15.3 copy-start.16
  1035.8 15.4 copy-start.55
  1035.8 15.4 copy-start.57
  1048.3 5.5 copy-start.61
  1048.4 5.5 copy-start.63
  1048.4 5.5 copy-start.62
  1048.4 5.5 copy-start.64
  1048.4 5.5 copy-start.60
  1048.4 5.6 copy-start.59
  1053.1 48.8 %copy-start.3 = (f32[564,384]{1,0:T(8,128)S(1)}, f32[564,384]{1,0:T(8,128)}, u32[]{:S(2)}) copy-start(f32[564,384]{1,0:T(8,128)} %copy-done.2) | copy-start | bytes 2598916
  1053.1 48.8 %copy-start.6 = (f32[564,384]{1,0:T(8,128)S(1)}, f32[564,384]{1,0:T(8,128)}, u32[]{:S(2)}) copy-start(f32[564,384]{1,0:T(8,128)} %reduce-scatter.12.cloned.1.call-done) | copy-start | bytes 2598916
  (35 other events, 102.7 us)
Sparse Core Ops, SparseCore 0:
  11.9 73.9 all-reduce.10
  88.7 107.3 all-gather.14
  198.2 18.7 all-gather.12
  219.6 51.8 all-gather.22
  276.5 38.4 reduce-scatter.5
  317.0 20.5 all-gather.18
  340.4 137.2 all-gather.26
  480.4 135.4 all-gather.24
  618.0 18.7 all-gather.16
  654.3 39.8 reduce-scatter.9
  697.4 39.8 reduce-scatter.7
  743.7 20.5 all-gather.20
  845.7 39.8 reduce-scatter.11
  918.4 570.0 all-reduce.12
  1492.6 1120.5 all-reduce.14
where the time goes:
time: 2640 us; the launch traced here: 2630 us
  waiting for transfers between devices  2070 us (78%)
  local copies, waits for them, and re-layouts  178 us (7%)
  matrix products  171 us (6%)
  other arithmetic  116 us (4%)
  blocking collectives  66.6 us (3%)
    unnamed x18, waiting for transfers between devices  1560 us
    all_gather x2, waiting for transfers between devices, fold_rows(): portion = lax.all_gather(weight, 'row', axis=0, tiled=True)  228 us
    all_gather x2, waiting for transfers between devices, map_rows(): portion = lax.all_gather(weight, 'row', axis=0, tiled=True)  162 us
    another operation x1, local copies, waits for them, and re-layouts, mlp_part(): return jnp.stack([image_part, text_part], axis=1)  55.5 us
  transfers between devices with their start and end apart: 15, of which 14 were waited for; matrix products, arithmetic and copies ran while one was open for 13% of the time, Pallas kernels for 0%

commit v1 on v0

--- a/solution.py
+++ b/solution.py
@@ -11,6 +11,23 @@
 TXT_DEV = 308
 EPSILON = 1e-06
 HIGHEST = lax.Precision.HIGHEST
+
+
+def _point_records(mine, d0):
+    e_now = list(mine.shape[1:])
+    e_now[d0] *= mine.shape[0]
+    return jnp.moveaxis(mine, 0, d0).reshape(e_now)
+
+
+def step_on_routes_all(local_array, a_name):
+    front, out_arr = (lax.axis_size(a_name), lax.axis_index(a_name))
+    z2, y1 = (local_array[None], 1)
+    while y1 < front:
+        next_value = lax.ppermute(z2, a_name, list(map(lambda j0: (j0, j0 ^ y1), range(front))))
+        passed = out_arr & y1 == 0
+        z2 = jnp.concatenate([jnp.where(passed, z2, next_value), jnp.where(passed, next_value, z2)])
+        y1 *= 2
+    return z2
 
 
 def slot_table(lengths, image_rows, text_rows):
@@ -122,7 +139,11 @@
 
 
 def map_rows(left, weight):
-    portion = lax.all_gather(weight, "row", axis=0, tiled=True)
+
+    def solve_sides(dimension_no, shard_in, field_in):
+        return _point_records(step_on_routes_all(field_in, shard_in), dimension_no)
+
+    portion = solve_sides(0, "row", weight)
     return stream_dot(left, portion[:, 0].T, portion[:, 1].T)
 
 

time: 2640 us -> 3260 us (1.23)
  waiting for transfers between devices: 2070 us -> 2500 us
  other arithmetic: 116 us -> 247 us
  local copies, waits for them, and re-layouts: 178 us -> 222 us
    ppermute x0 -> x12, waiting for transfers between devices: none -> 772 us  [step_on_routes_all(): lax.ppermute(z2, a_name, list(map(lambda j0: (j0, j0 ^ y1), range(front))))]
    all_gather x2 -> x0, waiting for transfers between devices: 162 us -> none  [map_rows(): portion = lax.all_gather(weight, 'row', axis=0, tiled=True)]
    concatenate x0 -> x12, other arithmetic: none -> 73.1 us  [step_on_routes_all(): jnp.concatenate([jnp.where(passed, z2, next_value), jnp.where(passed, nex...]
    select_n x0 -> x11, other arithmetic: none -> 57.6 us  [step_on_routes_all(): jnp.where(passed, z2, next_value)]
    reduce_scatter x2, waiting for transfers between devices: 51.9 us -> 0.01 us  [scatter_features(): return lax.psum_scatter(values, 'col', scatter_dimension=1, tiled=True)]
    all_gather x2 -> x4, waiting for transfers between devices: 228 us -> 177 us  [fold_rows(): portion = lax.all_gather(weight, 'row', axis=0, tiled=True)]
  transfers between devices with their start and end apart: 15 -> 27, of which waited for: 14 -> 17; matrix products, arithmetic and copies ran while one was open for 13% -> 15% of each run, Pallas kernels for 0% -> 0%
where the time goes in v1:
time: 3260 us; the launch traced here: 3240 us
  waiting for transfers between devices  2500 us (77%)
  other arithmetic  247 us (8%)
  local copies, waits for them, and re-layouts  222 us (7%)
  matrix products  168 us (5%)
  blocking collectives  64 us (2%)
    unnamed x18, waiting for transfers between devices  1550 us
    ppermute x12, waiting for transfers between devices, step_on_routes_all(): lax.ppermute(z2, a_name, list(map(lambda j0: (j0, j0 ^ y1), range(front))))  772 us
    all_gather x4, waiting for transfers between devices, fold_rows(): portion = lax.all_gather(weight, 'row', axis=0, tiled=True)  177 us
    concatenate x12, other arithmetic, step_on_routes_all(): jnp.concatenate([jnp.where(passed, z2, next_value), jnp.where(passed, nex...  73.1 us
  transfers between devices with their start and end apart: 27, of which 17 were waited for; matrix products, arithmetic and copies ran while one was open for 15% of the time, Pallas kernels for 0%

profile of v1, /device:TPU:0, one launch (start us, length us, event | category | flops | bytes accessed | tf_op | source)
XLA Modules:
  0.0 3242.0 jit_solution(10906370512133535611)
XLA Ops:
  17.7 8.0 collective-permute-done
  30.5 6.2 all-reduce.6
  36.9 7.4 collective-permute-done.1
  52.8 54.2 %all-reduce.11.cloned.1.call-done = f32[16,1,2,6,384]{4,0,3,2,1:T(8,128)} async-done(((f32[16,1,2,6,384]{4,0,3,2,1:T(8,128)}), f32[16,1,2,6,384]{4,0,3,2,1:T(8,128)}) %all-reduce.11.cloned.1.call-update) | async-done | bytes 294928
  123.6 94.0 %all-gather.15.cloned.1.call-done = bf16[1536,2,1152]{2,0,1:T(8,128)(2,1)} async-done(((bf16[192,2,1152]{2,0,1:T(8,128)(2,1)}), bf16[1536,2,1152]{2,0,1:T(8,128)(2,1)}) %all-gather.15.cloned.1.call-update) | async-done | bytes 7077904 | tf_op jit(solution)/shard_map/all_gather | solution.py:137
  217.6 6.6 slice_bitcast_fusion.21
  224.2 5.8 copy.192
  230.1 5.8 copy.191
  250.7 23.8 while.22
  292.8 25.7 collective-permute-done.6
  324.8 18.3 collective-permute-done.3
  349.4 66.0 %collective-permute-done.7 = bf16[2,192,2,1536]{3,2,1,0:T(2,128)(2,1)S(1)} collective-permute-done((bf16[2,192,2,1536]{3,2,1,0:T(2,128)(2,1)S(1)}, bf16[2,192,2,1536]{3,2,1,0:T(2,128)(2,1)S(1)}, u32[]{:S(2)}, u32[]{:S(2)}) %collective-permute-start.7) | collective-permute-done | bytes 2359328 | tf_op jit(solution)/shard_map/ppermute | solution.py:26
  415.4 110.3 %collective-permute-done.4 = bf16[2,192,2,1536]{3,2,1,0:T(2,128)(2,1)S(1)} collective-permute-done((bf16[2,192,2,1536]{3,2,1,0:T(2,128)(2,1)S(1)}, bf16[2,192,2,1536]{3,2,1,0:T(2,128)(2,1)S(1)}, u32[]{:S(2)}, u32[]{:S(2)}) %collective-permute-start.4) | collective-permute-done | bytes 2359328 | tf_op jit(solution)/shard_map/ppermute | solution.py:26
  525.7 13.3 broadcast_select_fusion.5
  539.0 10.6 pad_maximum_fusion.6
  563.3 10.9 pad_maximum_fusion.5
  575.0 387.9 %collective-permute-done.8 = bf16[4,192,2,1536]{3,2,1,0:T(2,128)(2,1)} collective-permute-done((bf16[4,192,2,1536]{3,2,1,0:T(2,128)(2,1)}, bf16[4,192,2,1536]{3,2,1,0:T(2,128)(2,1)}, u32[]{:S(2)}, u32[]{:S(2)}) %collective-permute-start.8) | collective-permute-done | bytes 4718624 | tf_op jit(solution)/shard_map/ppermute | solution.py:26
  962.8 13.0 broadcast_select_fusion.1
  977.7 6.2 all-reduce.5
  986.1 14.9 pad_maximum_fusion.3
  1001.0 9.3 copy.200
  1010.3 5.2 fusion.43
  1015.5 5.3 fusion.42
  1037.8 23.9 collective-permute-done.5
  1061.6 12.3 broadcast_select_fusion.3
  1073.9 13.6 pad_maximum_fusion.2
  1087.5 9.2 copy.198
  1110.2 18.1 collective-permute-done.9
  1134.6 46.8 %collective-permute-done.10 = bf16[2,192,2,1152]{3,1,2,0:T(8,128)(2,1)} collective-permute-done((bf16[2,192,2,1152]{3,1,2,0:T(8,128)(2,1)S(1)}, bf16[2,192,2,1152]{3,1,2,0:T(8,128)(2,1)}, u32[]{:S(2)}, u32[]{:S(2)}) %collective-permute-start.10) | collective-permute-done | bytes 1769504 | tf_op jit(solution)/shard_map/ppermute | solution.py:26
  1191.8 6.7 all-reduce.4
  1206.6 83.0 %all-gather.27.cloned.1.call-done = bf16[1,1536,2,384]{3,1,2,0:T(8,128)(2,1)} async-done(((bf16[1,192,2,384]{3,1,2,0:T(8,128)(2,1)}), bf16[1,1536,2,384]{3,1,2,0:T(8,128)(2,1)}) %all-gather.27.cloned.1.call-update) | async-done | bytes 2359312 | tf_op jit(solution)/shard_map/all_gather | solution.py:137
  1297.9 59.3 %collective-permute-done.11 = bf16[4,192,2,1152]{3,1,2,0:T(8,128)(2,1)} collective-permute-done((bf16[4,192,2,1152]{3,1,2,0:T(8,128)(2,1)}, bf16[4,192,2,1152]{3,1,2,0:T(8,128)(2,1)}, u32[]{:S(2)}, u32[]{:S(2)}) %collective-permute-start.11) | collective-permute-done | bytes 3538976 | tf_op jit(solution)/shard_map/ppermute | solution.py:26
  1362.3 6.7 pad_maximum_fusion.4
  1369.1 6.5 copy.211
  1380.2 69.1 %while.23 = (s32[]{:T(128)}, bf16[6,3,564,64]{2,3,0,1:T(8,128)(2,1)}, s32[564]{0:T(1024)S(1)}, bf16[6,564,64]{2,1,0:T(8,128)(2,1)}, bf16[6,564,64]{2,1,0:T(8,128...) while((s32[]{:T(128)}, ...), condition=%wide.region_27.28_spmd, body=%wide.region_25.27_spmd.sunk | while | flops 207346144 | bytes 8020453 | solution.py:323
  1474.6 8.4 maximum_bitcast_fusion.4
  1483.0 7.8 maximum_bitcast_fusion.3
  1490.8 14.6 pad_maximum_fusion.1
  1505.4 28.3 copy.216
  1552.3 7.8 maximum_bitcast_fusion.2
  1560.1 11.3 maximum_bitcast_fusion.1
  1571.4 21.2 pad_maximum_fusion
  1592.6 55.9 %copy.218 = f32[1536,2,3072]{2,1,0:T(2,128)} copy(f32[1536,2,3072]{0,2,1:T(8,128)} %pad_maximum_fusion) | data formatting | bytes 75497472 | tf_op jit(solution)/shard_map/stack | solution.py:166
  1669.4 33.0 %all-gather.3 = f32[16,2,6,384]{3,1,2,0:T(2,128)S(1)} all-gather(f32[2,2,6,384]{3,1,2,0:T(2,128)S(1)} %copy.212), channel_id=5, replica_groups=mesh['row'=8,'col'=4] {'row'}, dimensions={0}, use_global_device_ids=true | all-gather | bytes 331776 | tf_op jit(solution)/shard_map/all_gather | solution.py:352
  1704.6 11.9 all-reduce.3
  1726.7 375.9 %all-reduce.13.cloned.1.call-done = f32[1536,2,1536]{2,1,0:T(2,128)} async-done(((f32[1536,2,1536]{2,1,0:T(2,128)}), f32[1536,2,1536]{2,1,0:T(2,128)}) %all-reduce.13.cloned.1.call-update) | async-done | bytes 18874384
  2108.4 1118.8 %all-reduce.15.cloned.1.call-done = f32[1536,2,3072]{2,1,0:T(2,128)} async-done(((f32[1536,2,3072]{2,1,0:T(2,128)}), f32[1536,2,3072]{2,1,0:T(2,128)}) %all-reduce.15.cloned.1.call-update) | async-done | bytes 37748752
  3227.2 7.8 dynamic-slice_bitcast_fusion
  (456 shorter events, 350.7 us)
Async XLA Ops:
  7.2 99.7 %all-reduce.11.cloned.1.call-start = ((), (), s32[]{:S(2)}) async-start(), calls=%async_computation.16 | async-start | bytes 589824
  10.5 207.2 %all-gather.15.cloned.1.call-start = ((), (), s32[]{:S(2)}) async-start(), calls=%async_computation.5 | async-start | bytes 7962624 | tf_op jit(solution)/shard_map/all_gather | solution.py:137
  12.1 16.3 copy-start.3
  12.1 18.1 copy-start.24
  12.2 18.1 copy-start.25
  14.1 224.4 %all-gather.13.cloned.1.call-start = ((), (), s32[]{:S(2)}) async-start(), calls=%async_computation.4 | async-start | bytes 2181120 | tf_op jit(solution)/shard_map/all_gather | solution.py:112
  14.2 11.4 collective-permute-start
  17.5 537.6 %copy-start.57 = (s32[2]{0:T(128)}, s32[2]{0:T(128)S(1)}, u32[]{:S(2)}) copy-start(s32[2]{0:T(128)S(1)} %get-tuple-element.292) | copy-start | bytes 28
  17.5 537.6 %copy-start.59 = (s32[2]{0:T(128)}, s32[2]{0:T(128)S(1)}, u32[]{:S(2)}) copy-start(s32[2]{0:T(128)S(1)} %get-tuple-element.393) | copy-start | bytes 28
  17.5 543.5 %copy-start.61 = (s32[2]{0:T(128)}, s32[2]{0:T(128)S(1)}, u32[]{:S(2)}) copy-start(s32[2]{0:T(128)S(1)} %get-tuple-element.293) | copy-start | bytes 28
  17.6 543.5 %copy-start.63 = (s32[2]{0:T(128)}, s32[2]{0:T(128)S(1)}, u32[]{:S(2)}) copy-start(s32[2]{0:T(128)S(1)} %get-tuple-element.392) | copy-start | bytes 28
  28.5 15.8 collective-permute-start.1
  36.8 75.8 %copy-start.66 = (f32[564]{0:T(1024)}, f32[564]{0:T(1024)S(1)}, u32[]{:S(2)}) copy-start(f32[564]{0:T(1024)S(1)} %get-tuple-element.388) | copy-start | bytes 6772
  36.8 75.8 %copy-start.68 = (f32[564]{0:T(1024)}, f32[564]{0:T(1024)S(1)}, u32[]{:S(2)}) copy-start(f32[564]{0:T(1024)S(1)} %get-tuple-element.389) | copy-start | bytes 6772
  36.8 14.6 copy-start.80
  49.4 65.6 %collective-permute-start.2 = (bf16[4,192,2,384]{3,2,1,0:T(2,128)(2,1)}, bf16[4,192,2,384]{3,2,1,0:T(2,128)(2,1)}, u32[]{:S(2)}, u32[]{:S(2)}) collective-permute-start(bf16[4,192,2,384]{3,2,1,0:T(2,128)(2,1)} %pad_maximum_fusion.17), channel_id=1, source_target_pairs={{0,16},{4,20},{8,24},{12,28},{16,0},{20,4},{24,8},{28,12},{1,17},{... | collective-permute-start | bytes 3538952 | tf_op jit(solution)/shard_map/ppermute | solution.py:26
  114.5 861.3 %reduce-scatter.6.cloned.1.call-start = ((), (), s32[]{:S(2)}) async-start(), calls=%async_computation.6 | async-start | bytes 4362240 | tf_op jit(solution)/shard_map/reduce_scatter | solution.py:120
  281.8 728.5 %all-gather.19.cloned.1.call-start = ((), (), s32[]{:S(2)}) async-start(), calls=%async_computation.9 | async-start | bytes 2181120 | tf_op jit(solution)/shard_map/all_gather | solution.py:116
  286.5 723.7 %all-gather.25.cloned.1.call-start = ((), (), s32[]{:S(2)}) async-start(), calls=%async_computation.14 | async-start | bytes 10616832 | tf_op jit(solution)/shard_map/all_gather | solution.py:137
  289.5 731.3 %all-gather.23.cloned.1.call-start = ((), (), s32[]{:S(2)}) async-start(), calls=%async_computation.13 | async-start | bytes 10616832 | tf_op jit(solution)/shard_map/all_gather | solution.py:137
  289.5 29.0 collective-permute-start.6
  291.0 52.1 %collective-permute-start.3 = (bf16[1,192,2,1536]{3,2,1,0:T(2,128)(2,1)}, bf16[1,192,2,1536]{3,2,1,0:T(2,128)(2,1)}, u32[]{:S(2)}, u32[]{:S(2)}) collective-permute-start(bf16[1,192,2,1536]{3,2,1,0:T(2,128)(2,1)} %param.23), channel_id=1, source_target_pairs={{0,4},{4,0},{8,12},{12,8},{16,20},{20,16},{24,28},{28,24},{1,5},{5... | collective-permute-start | bytes 3538952 | tf_op jit(solution)/shard_map/ppermute | solution.py:26
  292.8 728.0 %all-gather.17.cloned.1.call-start = ((), (), s32[]{:S(2)}) async-start(), calls=%async_computation.7 | async-start | bytes 2181120 | tf_op jit(solution)/shard_map/all_gather | solution.py:112
  320.0 23.2 copy-start.27
  323.3 92.1 %collective-permute-start.7 = (bf16[2,192,2,1536]{3,2,1,0:T(2,128)(2,1)S(1)}, bf16[2,192,2,1536]{3,2,1,0:T(2,128)(2,1)S(1)}, u32[]{:S(2)}, u32[]{:S(2)}) collective-permute-start(bf16[2,192,2,1536]{3,2,1,0:T(2,128)(2,1)S(1)} %pad_maximum_fusion.15), channel_id=1, source_target_pairs={{0,8},{4,12},{8,0},{12,4},{16,24},{20,28},{24,16},{28,20},{1,9},{5... | collective-permute-start | bytes 7077896 | tf_op jit(solution)/shard_map/ppermute | solution.py:26
  347.9 177.8 %collective-permute-start.4 = (bf16[2,192,2,1536]{3,2,1,0:T(2,128)(2,1)S(1)}, bf16[2,192,2,1536]{3,2,1,0:T(2,128)(2,1)S(1)}, u32[]{:S(2)}, u32[]{:S(2)}) collective-permute-start(bf16[2,192,2,1536]{3,2,1,0:T(2,128)(2,1)S(1)} %pad_maximum_fusion.14), channel_id=1, source_target_pairs={{0,8},{4,12},{8,0},{12,4},{16,24},{20,28},{24,16},{28,20},{1,9},{5... | collective-permute-start | bytes 7077896 | tf_op jit(solution)/shard_map/ppermute | solution.py:26
  549.6 413.3 %collective-permute-start.8 = (bf16[4,192,2,1536]{3,2,1,0:T(2,128)(2,1)}, bf16[4,192,2,1536]{3,2,1,0:T(2,128)(2,1)}, u32[]{:S(2)}, u32[]{:S(2)}) collective-permute-start(bf16[4,192,2,1536]{3,2,1,0:T(2,128)(2,1)} %pad_maximum_fusion.6), channel_id=1, source_target_pairs={{0,16},{4,20},{8,24},{12,28},{16,0},{20,4},{24,8},{28,12},{1,17},{... | collective-permute-start | bytes 14155784 | tf_op jit(solution)/shard_map/ppermute | solution.py:26
  555.1 428.7 %copy-start.20 = (f32[256,384]{1,0:T(8,128)}, f32[256,384]{1,0:T(8,128)S(1)}, u32[]{:S(2)}) copy-start(f32[256,384]{1,0:T(8,128)S(1)} %fusion.188) | copy-start | bytes 1179652
  561.0 422.8 %copy-start.13 = (f32[308,384]{1,0:T(8,128)}, f32[308,384]{1,0:T(8,128)S(1)}, u32[]{:S(2)}) copy-start(f32[308,384]{1,0:T(8,128)S(1)} %fusion.155) | copy-start | bytes 1419268
  574.2 487.4 %collective-permute-start.5 = (bf16[4,192,2,1536]{3,2,1,0:T(2,128)(2,1)}, bf16[4,192,2,1536]{3,2,1,0:T(2,128)(2,1)}, u32[]{:S(2)}, u32[]{:S(2)}) collective-permute-start(bf16[4,192,2,1536]{3,2,1,0:T(2,128)(2,1)} %pad_maximum_fusion.5), channel_id=1, source_target_pairs={{0,16},{4,20},{8,24},{12,28},{16,0},{20,4},{24,8},{28,12},{1,17},{... | collective-permute-start | bytes 14155784 | tf_op jit(solution)/shard_map/ppermute | solution.py:26
  977.6 23.3 copy-start.2
  986.1 203.5 %reduce-scatter.10.cloned.1.call-start = ((), (), s32[]{:S(2)}) async-start(), calls=%async_computation.10 | async-start | bytes 4362240 | tf_op jit(solution)/shard_map/reduce_scatter | solution.py:124
  1032.5 68.2 %copy-start.18 = (bf16[564,1536]{1,0:T(8,128)(2,1)}, bf16[564,1536]{1,0:T(8,128)(2,1)S(1)}, u32[]{:S(2)}) copy-start(bf16[564,1536]{1,0:T(8,128)(2,1)S(1)} %get-tuple-element.361) | copy-start | bytes 5197828
  1037.7 162.2 %reduce-scatter.8.cloned.1.call-start = ((), (), s32[]{:S(2)}) async-start(), calls=%async_computation.8 | async-start | bytes 4362240 | tf_op jit(solution)/shard_map/reduce_scatter | solution.py:120
  1105.6 184.0 %all-gather.27.cloned.1.call-start = ((), (), s32[]{:S(2)}) async-start(), calls=%async_computation.15 | async-start | bytes 2654208 | tf_op jit(solution)/shard_map/all_gather | solution.py:137
  1108.8 19.5 collective-permute-start.9
  1130.8 50.6 %collective-permute-start.10 = (bf16[2,192,2,1152]{3,1,2,0:T(8,128)(2,1)S(1)}, bf16[2,192,2,1152]{3,1,2,0:T(8,128)(2,1)}, u32[]{:S(2)}, u32[]{:S(2)}) collective-permute-start(bf16[2,192,2,1152]{3,1,2,0:T(8,128)(2,1)S(1)} %pad_maximum_fusion.16), channel_id=1, source_target_pairs={{0,8},{4,12},{8,0},{12,4},{16,24},{20,28},{24,16},{28,20},{1,9},{5... | collective-permute-start | bytes 5308424 | tf_op jit(solution)/shard_map/ppermute | solution.py:26
  1134.5 241.1 %all-gather.21.cloned.1.call-start = ((), (), s32[]{:S(2)}) async-start(), calls=%async_computation.11 | async-start | bytes 2181120 | tf_op jit(solution)/shard_map/all_gather | solution.py:116
  1186.1 171.1 %collective-permute-start.11 = (bf16[4,192,2,1152]{3,1,2,0:T(8,128)(2,1)}, bf16[4,192,2,1152]{3,1,2,0:T(8,128)(2,1)}, u32[]{:S(2)}, u32[]{:S(2)}) collective-permute-start(bf16[4,192,2,1152]{3,1,2,0:T(8,128)(2,1)} %pad_maximum_fusion.7), channel_id=1, source_target_pairs={{0,16},{4,20},{8,24},{12,28},{16,0},{20,4},{24,8},{28,12},{1,17},{... | collective-permute-start | bytes 10616840 | tf_op jit(solution)/shard_map/ppermute | solution.py:26
  1206.6 457.2 %reduce-scatter.12.cloned.1.call-start = ((), (), s32[]{:S(2)}) async-start(), calls=%async_computation.12 | async-start | bytes 4362240 | tf_op jit(solution)/shard_map/reduce_scatter | solution.py:124
  1461.0 641.5 %all-reduce.13.cloned.1.call-start = ((), (), s32[]{:S(2)}) async-start(), calls=%async_computation.17 | async-start | bytes 37748736
  1533.7 1693.5 %all-reduce.15.cloned.1.call-start = ((), (), s32[]{:S(2)}) async-start(), calls=%async_computation.18 | async-start | bytes 75497472
  1651.3 15.3 copy-start.15
  1651.3 15.3 copy-start.22
  1651.3 15.4 copy-start.67
  1651.3 15.4 copy-start.69
  1668.5 48.0 %copy-start.10 = (f32[564,384]{1,0:T(8,128)S(1)}, f32[564,384]{1,0:T(8,128)}, u32[]{:S(2)}) copy-start(f32[564,384]{1,0:T(8,128)} %copy-done.9) | copy-start | bytes 2598916
  1668.5 48.0 %copy-start.12 = (f32[564,384]{1,0:T(8,128)S(1)}, f32[564,384]{1,0:T(8,128)}, u32[]{:S(2)}) copy-start(f32[564,384]{1,0:T(8,128)} %reduce-scatter.12.cloned.1.call-done) | copy-start | bytes 2598916
  (63 other events, 247.2 us)
Sparse Core Ops, SparseCore 0:
  11.9 94.9 all-reduce.10
  109.7 107.8 all-gather.14
  219.8 18.7 all-gather.12
  281.9 39.9 reduce-scatter.5
  323.3 20.5 all-gather.18
  346.5 193.6 all-gather.24
  542.3 383.3 all-gather.22
  986.2 19.4 all-gather.16
  1037.8 38.8 reduce-scatter.9
  1105.7 40.0 reduce-scatter.7
  1148.5 141.0 all-gather.26
  1291.6 20.9 all-gather.20
  1461.1 38.9 reduce-scatter.11
  1533.9 568.6 all-reduce.12
  2106.6 1120.5 all-reduce.14
